TPU v7x, 32 devices: a whole 2x2x4 slice. The times are simulated.
32 devices in a mesh: groups: 2 (over y), prompt: 4 (over z), sample: 2 (over x), head: 2 (over core).
Axes of the slice: x: 2, y: 2, z: 4, core: 2. Of those that a mesh axis runs over, the one named last changes fastest.
Arguments:
- queries: bfloat16 [256, 16, 576], P(('groups', 'prompt', 'sample'), 'head'), parts along dimension 0, may hold values from -6 to 6
- prompt_cache: bfloat16 [16, 1024, 576], P(('groups', 'prompt'), 'sample'), parts along dimension 0, may hold values from -6 to 6
- suffix_cache: bfloat16 [256, 64, 576], P(('groups', 'prompt', 'sample')), parts along dimension 0, may hold values from -6 to 6
- suffix_len: int32 [256], P(('groups', 'prompt', 'sample')), parts along dimension 0, may hold values from 2 to 64, as said below
- sample_prompt: int32 [256], P('groups'), parts along dimension 0, may hold values from 0 to 7, as said below
- prompt_slot: int32 [16], P('groups'), parts along dimension 0, may hold values from 0 to 7, as said below
Outputs:
- attended: bfloat16 [256, 16, 512], P(('groups', 'prompt', 'sample'), 'head'), parts along dimension 0
There are 2 independent parts, one for each index of `groups`. A program takes and returns all parts, laid end to end along the dimension named above; each array names one. Nothing has to cross between parts.
Inputs may be any that keep to these rules, and one draw needn't show every extreme that they name: `suffix_len`: the value 64 is reached. Every prompt is named by exactly 16 samples; in each aligned block of 16 samples, prompt_slot[sample_prompt] // 2 takes no value more than 4 times, and some value exactly 4 times. `prompt_slot`: a permutation.
All inputs are finite; a program needn't handle non-finite values.
Results may differ from a plain program's by a relative error of at most 0.013.
Values may be sent and summed in bfloat16 or wider, within the bound.
A program may use at most 64 MiB of HBM per device.

v0:
```python
import math

import jax
import jax.numpy as jnp
from jax import lax
from jax.sharding import PartitionSpec as P

DL = 512
DR = 64
QKN = 128
SPP = 16
P_DEV = 2


def partial_softmax(asked, keys, score_form, value_form, scaling, allowed):
    scores = jnp.einsum(score_form, asked, keys, preferred_element_type=jnp.float32) * scaling
    if allowed is not None:
        scores = jnp.where(allowed, scores, -1e30)
    row_max = jnp.max(scores, axis=-1)
    weights = jnp.exp(scores - row_max[..., None])
    row_sum = jnp.sum(weights, axis=-1)
    row_out = jnp.einsum(
        value_form, weights.astype(jnp.bfloat16), keys[..., :DL], preferred_element_type=jnp.float32
    )
    return (row_max, row_sum, row_out)


def routing_tables(sample_prompt, prompt_slot, device_count, per_device, owner_count, send_count):
    slot_index = jnp.take(prompt_slot, sample_prompt)
    owner_of = (slot_index // P_DEV).reshape(device_count, per_device)
    local_prompt = slot_index % P_DEV
    owners = jnp.arange(owner_count, dtype=jnp.int32)
    owner_hot = (owner_of[:, :, None] == owners[None, None, :]).astype(jnp.int32)
    rank_in = jnp.sum((jnp.cumsum(owner_hot, axis=1) - 1) * owner_hot, axis=2)
    places = jnp.arange(send_count, dtype=jnp.int32)
    matches = (owner_of[:, :, None, None] == owners[None, None, :, None]) & (
        rank_in[:, :, None, None] == places[None, None, None, :]
    )
    counter = jnp.arange(per_device, dtype=jnp.int32)[None, :, None, None]
    positions = jnp.sum(matches.astype(jnp.int32) * counter, axis=1)
    present = jnp.any(matches, axis=1)
    return (owner_of, rank_in, positions, present, local_prompt)


def prefix_partials(rows, row_samples, row_valid, local_prompt, prompt_cache, head_count, scaling):
    row_count = rows.shape[0]
    group_count = P_DEV * SPP
    feature_count = prompt_cache.shape[2]
    row_prompt = jnp.take(local_prompt, row_samples)
    prompt_hot = (
        (row_prompt[:, None] == jnp.arange(P_DEV, dtype=jnp.int32)[None, :]) & row_valid[:, None]
    ).astype(jnp.int32)
    prompt_rank = jnp.sum((jnp.cumsum(prompt_hot, axis=0) - 1) * prompt_hot, axis=1)
    grouped_at = row_prompt * SPP + prompt_rank
    marked = jnp.where(row_valid, grouped_at, -1)
    fetch_at = jnp.where(row_valid, grouped_at, 0)
    counter = jnp.arange(row_count, dtype=jnp.int32)
    places = jnp.arange(group_count, dtype=jnp.int32)
    source_row = jnp.sum(
        (marked[None, :] == places[:, None]).astype(jnp.int32) * counter[None, :], axis=1
    )
    grouped = jnp.take(rows, source_row, axis=0).reshape(P_DEV, SPP, head_count, feature_count)
    row_max, row_sum, row_out = partial_softmax(
        grouped, prompt_cache, "kshf,ktf->ksht", "ksht,ktd->kshd", scaling, None
    )
    row_max = jnp.take(row_max.reshape(group_count, head_count), fetch_at, axis=0)
    row_sum = jnp.take(row_sum.reshape(group_count, head_count), fetch_at, axis=0)
    row_out = jnp.take(row_out.reshape(group_count, head_count, DL), fetch_at, axis=0)
    return (row_max, row_sum, row_out)


def body(queries, prompt_cache, suffix_cache, suffix_len, sample_prompt, prompt_slot):
    per_device, head_count, feature_count = queries.shape
    owner_count = lax.axis_size("prompt")
    slice_count = lax.axis_size("sample")
    device_count = owner_count * slice_count
    send_count = max(1, per_device // owner_count)
    row_width = head_count * feature_count
    scaling = 1.0 / math.sqrt(QKN + DR)
    owner_of, rank_in, positions, present, local_prompt = routing_tables(
        sample_prompt, prompt_slot, device_count, per_device, owner_count, send_count
    )
    device = lax.axis_index(("prompt", "sample"))
    owner_index = lax.axis_index("prompt")
    flat_queries = queries.reshape(per_device, row_width)
    send_rows = lax.dynamic_index_in_dim(positions, device, 0, keepdims=False).reshape(-1)
    outgoing = jnp.take(flat_queries, send_rows, axis=0).reshape(owner_count, send_count, row_width)
    arrive_pos = lax.dynamic_index_in_dim(positions, owner_index, 1, keepdims=False)
    arrive_valid = lax.dynamic_index_in_dim(present, owner_index, 1, keepdims=False)
    arrive_ids = jnp.arange(device_count, dtype=jnp.int32)[:, None] * per_device + arrive_pos
    fanned = jnp.broadcast_to(outgoing[:, None], (owner_count, slice_count, send_count, row_width))
    fanned = fanned.reshape(device_count * send_count, row_width)
    arrived = lax.all_to_all(fanned, ("prompt", "sample"), split_axis=0, concat_axis=0, tiled=True)
    partials = prefix_partials(
        arrived,
        arrive_ids.reshape(-1),
        arrive_valid.reshape(-1),
        local_prompt,
        prompt_cache,
        head_count,
        scaling,
    )
    back_max, back_sum, back_out = (
        lax.all_to_all(partials[0], ("prompt", "sample"), split_axis=0, concat_axis=0, tiled=True),
        lax.all_to_all(partials[1], ("prompt", "sample"), split_axis=0, concat_axis=0, tiled=True),
        lax.all_to_all(partials[2], ("prompt", "sample"), split_axis=0, concat_axis=0, tiled=True),
    )
    back_max = back_max.reshape(owner_count, slice_count, send_count, head_count)
    back_sum = back_sum.reshape(owner_count, slice_count, send_count, head_count)
    back_out = back_out.reshape(owner_count, slice_count, send_count, head_count, DL)
    prefix_max = jnp.max(back_max, axis=1)
    rescale = jnp.exp(back_max - prefix_max[:, None])
    prefix_sum = jnp.sum(back_sum * rescale, axis=1)
    prefix_out = jnp.sum(back_out * rescale[..., None], axis=1)
    prefix_max = prefix_max.reshape(owner_count * send_count, head_count)
    prefix_sum = prefix_sum.reshape(owner_count * send_count, head_count)
    prefix_out = prefix_out.reshape(owner_count * send_count, head_count, DL)
    own_owner = lax.dynamic_index_in_dim(owner_of, device, 0, keepdims=False)
    own_rank = lax.dynamic_index_in_dim(rank_in, device, 0, keepdims=False)
    own_at = own_owner * send_count + own_rank
    pre_max = jnp.take(prefix_max, own_at, axis=0)
    pre_sum = jnp.take(prefix_sum, own_at, axis=0)
    pre_out = jnp.take(prefix_out, own_at, axis=0)
    suffix_tokens = suffix_cache.shape[1]
    allowed = (jnp.arange(suffix_tokens, dtype=jnp.int32)[None, :] < suffix_len[:, None])[
        :, None, :
    ]
    suf_max, suf_sum, suf_out = partial_softmax(
        queries, suffix_cache, "shf,stf->sht", "sht,std->shd", scaling, allowed
    )
    both_max = jnp.maximum(pre_max, suf_max)
    weight_pre = jnp.exp(pre_max - both_max)
    weight_suf = jnp.exp(suf_max - both_max)
    numerator = weight_pre[..., None] * pre_out + weight_suf[..., None] * suf_out
    denominator = weight_pre * pre_sum + weight_suf * suf_sum
    return (numerator / denominator[..., None]).astype(jnp.bfloat16)


def solution(mesh):
    return jax.shard_map(
        body,
        mesh=mesh,
        in_specs=(
            P(("groups", "prompt", "sample"), "head", None),
            P(("groups", "prompt"), "sample", None),
            P(("groups", "prompt", "sample"), None, None),
            P(("groups", "prompt", "sample")),
            P("groups"),
            P("groups"),
        ),
        out_specs=P(("groups", "prompt", "sample"), "head", None),
        check_vma=False,
    )
```

profile of v0, /device:TPU:0, one launch (start us, length us, event | category | flops | bytes accessed | tf_op | source)
XLA Modules:
  0.0 70.8 jit_solution(7681496976112053632)
XLA Ops:
  0.0 1.6 %fusion.42 = (s32[1]{0:T(128)}, s32[1]{0:T(128)}, s32[1]{0:T(128)}, s32[1]{0:T(128)}, s32[1]{0:T(128)}, /*index=5*/s32[1]{0:T(128)}, s32[1]{0:T(128)}, s32[1]{0:T(128)}) fusion(s32[8]{0:T(128)} %param.15), kind=kLoop, calls=%fused_computation.120 | loop fusion | bytes 64 | tf_op jit(solution)/shard_map/jit(_take)/gather | solution.py:29
  1.6 5.6 %and_select_fusion.2 = (s32[128]{0:T(128)S(1)}, s32[128]{0:T(128)S(1)}) fusion(s32[]{:T(128)} %bitcast.7, s32[]{:T(128)} %bitcast.6, s32[]{:T(128)} %bitcast.5, s32[]{:T(128)} %bitcast.4, s32[]{:T(128)} %bitcast.3, s32[]{:T(128)} %bitcast.2, s32[]{:T(128)} %bitcast.1, s32[]{:T(128)} %bitcast, s32[128]{0:T(128)} %param.14), kind=kLoop, calls=%fused_computation.103 | loop fusion | flops 4096 | bytes 1568 | tf_op jit(solution)/shard_map/jit(remainder)/select_n | solution.py:31
  7.2 0.1 select_n.229
  7.3 0.1 copy.38
  7.4 0.4 fusion.43
  7.8 0.1 iota_compare_fusion
  7.9 0.1 copy.43
  8.0 0.1 copy.42
  8.1 0.4 fusion.17
  8.5 0.2 dynamic-slice_reduce_fusion
  8.7 0.1 reshape.429
  8.9 1.1 %reshape.428 = bf16[16,4608]{1,0:T(8,128)(2,1)S(1)} reshape(bf16[16,8,576]{2,1,0:T(8,128)(2,1)} %param.10) | data formatting | bytes 294912 | tf_op jit(solution)/shard_map/reshape | solution.py:85
  10.0 0.6 gather_fusion.1
  10.7 0.1 broadcast_select_fusion.1
  10.8 0.8 %broadcast_in_dim.124 = bf16[4,2,4,4608]{3,2,1,0:T(4,128)(2,1)} broadcast(bf16[4,4,4608]{2,1,0:T(4,128)(2,1)S(1)} %broadcast_select_fusion.1), dimensions={0,2,3} | broadcast | bytes 442368 | tf_op jit(solution)/shard_map/broadcast_in_dim | solution.py:91
  11.6 7.3 %all-to-all-start = ((bf16[8,4,4608]{2,1,0:T(4,128)(2,1)}), bf16[8,4,4608]{2,1,0:T(4,128)(2,1)S(1)}, u32[]{:S(2)}, u32[]{:S(2)}) async-start(bf16[8,4,4608]{2,1,0:T(4,128)(2,1)} %bitcast.10), calls=%async_computation | async-start | bytes 589824 | tf_op jit(solution)/shard_map/all_to_all | solution.py:93
  18.9 0.1 copy.45
  19.0 0.1 squeeze.14
  19.1 0.1 squeeze.13
  19.1 0.1 add.241
  19.2 0.1 add.247
  19.3 0.1 add.242
  19.4 0.4 and_reduce_fusion
  19.8 0.1 copy.44
  19.9 0.1 reshape.426
  20.0 0.7 gather_fusion
  20.7 0.1 fusion.25
  20.8 0.2 select_reduce_fusion.1
  21.0 0.1 select_reduce_fusion
  21.2 0.1 reduce_sum.82
  21.3 0.2 add_reduce_fusion
  21.5 0.1 reshape.434
  21.5 0.6 fusion.35
  22.2 0.6 pad_clamp_fusion.2
  22.8 0.6 pad_clamp_fusion.1
  23.4 0.1 iota_compare_fusion.4
  23.5 1.7 %fusion.45 = (f32[16,8]{1,0:T(8,128)}, f32[16,8,64]{2,1,0:T(8,128)}) fusion(bf16[16,8,576]{2,1,0:T(8,128)(2,1)S(1)} %copy-done.2, bf16[16,64,576]{2,1,0:T(8,128)(2,1)S(1)} %copy-done.1, pred[16,64]{1,0:T(8,128)(4,1)S(1)} %iota_compare_fusion.4), kind=kOutput, calls=%fused_computation.123 | convolution fusion | flops 9461632 | bytes 1361408 | tf_op jit(solution)/shard_map/shf,stf->sht/dot_general | solution.py:16
  25.2 3.3 %all-to-all-done = bf16[8,4,4608]{2,1,0:T(4,128)(2,1)S(1)} async-done(((bf16[8,4,4608]{2,1,0:T(4,128)(2,1)}), bf16[8,4,4608]{2,1,0:T(4,128)(2,1)S(1)}, u32[]{:S(2)}, u32[]{:S(2)}) %all-to-all-start) | async-done | bytes 294944 | tf_op jit(solution)/shard_map/all_to_all | solution.py:93
  28.5 0.1 all_to_all.25
  28.6 1.4 %gather_fusion.2 = bf16[32,4608]{1,0:T(8,128)(2,1)} fusion(bf16[32,4608]{1,0:T(8,128)(2,1)S(1)} %all_to_all.25, s32[1024]{0:T(1024)S(1)} %pad_clamp_fusion.4), kind=kCustom, calls=%fused_computation.6 | custom fusion | bytes 589952 | tf_op jit(solution)/shard_map/jit(_take)/gather | solution.py:62
  30.0 1.2 %gather.41 = bf16[2,16,8,576]{3,2,1,0:T(8,128)(2,1)S(1)} reshape(bf16[32,4608]{1,0:T(8,128)(2,1)} %gather_fusion.2) | data formatting | bytes 589824 | tf_op jit(solution)/shard_map/jit(_take)/gather | solution.py:62
  31.3 0.5 fusion.44
  31.8 0.2 fusion.10
  32.0 0.6 gather_fusion.7
  32.6 0.6 gather_fusion.5
  33.2 0.7 broadcast_select_fusion.3
  33.8 4.0 %all-to-all-start.1 = ((f32[8,4,8]{2,1,0:T(4,128)}), f32[8,4,8]{2,1,0:T(4,128)}, u32[]{:S(2)}, u32[]{:S(2)}) async-start(f32[8,4,8]{2,1,0:T(4,128)} %bitcast.16), calls=%async_computation.1 | async-start | bytes 32768 | tf_op jit(solution)/shard_map/all_to_all | solution.py:104
  37.8 0.5 fusion.6
  38.3 0.7 %gather_fusion.3 = f32[32,8,512]{2,1,0:T(8,128)S(1)} fusion(f32[32,8,512]{2,1,0:T(8,128)S(1)} %bitcast.74, s32[1024]{0:T(1024)} %pad_clamp_fusion.1), kind=kCustom, calls=%fused_computation.7 | custom fusion | bytes 1048704 | tf_op jit(solution)/shard_map/jit(_take)/gather | solution.py:68
  39.0 5.3 %all-to-all-done.1 = f32[8,4,8]{2,1,0:T(4,128)} async-done(((f32[8,4,8]{2,1,0:T(4,128)}), f32[8,4,8]{2,1,0:T(4,128)}, u32[]{:S(2)}, u32[]{:S(2)}) %all-to-all-start.1) | async-done | bytes 1056 | tf_op jit(solution)/shard_map/all_to_all | solution.py:104
  44.4 3.3 %all-to-all-start.3 = ((f32[8,4,8]{2,1,0:T(4,128)}), f32[8,4,8]{2,1,0:T(4,128)S(1)}, u32[]{:S(2)}, u32[]{:S(2)}) async-start(f32[8,4,8]{2,1,0:T(4,128)} %bitcast.80), calls=%async_computation.3 | async-start | bytes 32768 | tf_op jit(solution)/shard_map/all_to_all | solution.py:105
  47.7 1.6 %broadcast_select_fusion = f32[32,8,512]{2,1,0:T(8,128)} fusion(f32[32,8,512]{2,1,0:T(8,128)S(1)} %gather_fusion.3, pred[32]{0:T(512)(128)(4,1)} %copy-done.5), kind=kLoop, calls=%fused_computation.29 | loop fusion | flops 131072 | bytes 1048608 | tf_op jit(solution)/shard_map/jit(_take)/select_n | solution.py:68
  49.3 5.0 %all-to-all-done.3 = f32[8,4,8]{2,1,0:T(4,128)S(1)} async-done(((f32[8,4,8]{2,1,0:T(4,128)}), f32[8,4,8]{2,1,0:T(4,128)S(1)}, u32[]{:S(2)}, u32[]{:S(2)}) %all-to-all-start.3) | async-done | bytes 1056 | tf_op jit(solution)/shard_map/all_to_all | solution.py:105
  54.2 3.5 %all-to-all-start.2 = ((f32[32,8,512]{2,1,0:T(8,128)}), f32[32,8,512]{2,1,0:T(8,128)S(1)}, u32[]{:S(2)}, u32[]{:S(2)}) async-start(f32[32,8,512]{2,1,0:T(8,128)} %broadcast_select_fusion), calls=%async_computation.2 | async-start | bytes 1048576 | tf_op jit(solution)/shard_map/all_to_all | solution.py:106
  57.8 0.2 fusion.19
  58.0 0.7 %bitcast_reduce_fusion = f32[4,4,8]{2,1,0:T(4,128)S(1)} fusion(f32[8,4,8]{2,1,0:T(4,128)} %all-to-all-done.1), kind=kLoop, calls=%fused_computation.43 | loop fusion | flops 128 | bytes 1536 | tf_op jit(solution)/shard_map/reduce_max | solution.py:111
  58.7 0.7 %multiply_reduce_fusion.1 = (f32[4,4,8]{2,1,0:T(4,128)S(1)}, f32[4,2,4,8]{3,2,1,0:T(4,128)S(1)}) fusion(f32[8,4,8]{2,1,0:T(4,128)S(1)} %all-to-all-done.3, f32[4,4,8]{2,1,0:T(4,128)S(1)} %bitcast_reduce_fusion, f32[8,4,8]{2,1,0:T(4,128)} %all-to-all-done.1), kind=kLoop, calls=%fused_computation.45 | loop fusion | flops 640 | bytes 4096 | tf_op jit(solution)/shard_map/reduce_sum | solution.py:113
  59.5 0.7 gather_fusion.8
  60.1 0.7 gather_fusion.6
  60.8 0.1 fusion.29
  60.9 8.3 %all-to-all-done.2 = f32[32,8,512]{2,1,0:T(8,128)S(1)} async-done(((f32[32,8,512]{2,1,0:T(8,128)}), f32[32,8,512]{2,1,0:T(8,128)S(1)}, u32[]{:S(2)}, u32[]{:S(2)}) %all-to-all-start.2) | async-done | bytes 524320 | tf_op jit(solution)/shard_map/all_to_all | solution.py:106
  69.2 0.1 multiply_reduce_fusion
  69.3 0.6 gather_fusion.4
  69.9 1.0 %fusion.3 = bf16[16,8,512]{2,1,0:T(8,128)(2,1)} fusion(bf16[16,64,576]{2,1,0:T(8,128)(2,1)S(1)} %copy-done.1, f32[16,8,512]{2,1,0:T(8,128)S(1)} %gather_fusion.4, f32[16,8]{1,0:T(8,128)S(1)} %get-tuple-element.6, f32[16,8]{1,0:T(8,128)S(1)} %get-tuple-element.8, f32[16,8]{1,0:T(8,128)S(1)} %get-tuple-element.9, pred[16]{0:T(512)(128)(4,1)S(1)} %compare_and_fusion, ...), kind=kOutput, calls=%fused_computation.14 | convolution fusion | flops 8798208 | bytes 1540608 | tf_op jit(solution)/shard_map/sht,std->shd/dot_general | solution.py:22
  (43 shorter events, 0.3 us)
Async XLA Ops:
  10.6 12.8 %copy-start.6 = (s32[16]{0:T(128)S(1)}, s32[16]{0:T(128)}, u32[]{:S(2)}) copy-start(s32[16]{0:T(128)} %param.13) | copy-start | bytes 196
  10.6 12.8 %copy-start.1 = (bf16[16,64,576]{2,1,0:T(8,128)(2,1)S(1)}, bf16[16,64,576]{2,1,0:T(8,128)(2,1)}, u32[]{:S(2)}) copy-start(bf16[16,64,576]{2,1,0:T(8,128)(2,1)} %param.12) | copy-start | bytes 3538948
  10.6 12.8 %copy-start.2 = (bf16[16,8,576]{2,1,0:T(8,128)(2,1)S(1)}, bf16[16,8,576]{2,1,0:T(8,128)(2,1)}, u32[]{:S(2)}) copy-start(bf16[16,8,576]{2,1,0:T(8,128)(2,1)} %param.10) | copy-start | bytes 442372
  11.6 16.9 %all-to-all-start = ((bf16[8,4,4608]{2,1,0:T(4,128)(2,1)}), bf16[8,4,4608]{2,1,0:T(4,128)(2,1)S(1)}, u32[]{:S(2)}, u32[]{:S(2)}) async-start(bf16[8,4,4608]{2,1,0:T(4,128)(2,1)} %bitcast.10), calls=%async_computation | async-start | bytes 589824 | tf_op jit(solution)/shard_map/all_to_all | solution.py:93
  21.3 11.9 %copy-start.5 = (pred[32]{0:T(512)(128)(4,1)}, pred[32]{0:T(512)(128)(4,1)S(1)}, u32[]{:S(2)}) copy-start(pred[32]{0:T(512)(128)(4,1)S(1)} %get-tuple-element.12) | copy-start | bytes 100
  21.4 7.0 %copy-start.7 = (s32[16]{0:T(128)}, s32[16]{0:T(128)S(1)}, u32[]{:S(2)}) copy-start(s32[16]{0:T(128)S(1)} %add_reduce_fusion) | copy-start | bytes 196
  28.6 2.7 %copy-start = (bf16[2,512,576]{1,2,0:T(8,128)(2,1)S(1)}, bf16[2,512,576]{1,2,0:T(8,128)(2,1)}, u32[]{:S(2)}) copy-start(bf16[2,512,576]{1,2,0:T(8,128)(2,1)} %param.11) | copy-start | bytes 3538948
  33.8 10.6 %all-to-all-start.1 = ((f32[8,4,8]{2,1,0:T(4,128)}), f32[8,4,8]{2,1,0:T(4,128)}, u32[]{:S(2)}, u32[]{:S(2)}) async-start(f32[8,4,8]{2,1,0:T(4,128)} %bitcast.16), calls=%async_computation.1 | async-start | bytes 32768 | tf_op jit(solution)/shard_map/all_to_all | solution.py:104
  39.0 18.7 %copy-start.9 = (s32[16]{0:T(128)S(1)}, s32[16]{0:T(128)}, u32[]{:S(2)}) copy-start(s32[16]{0:T(128)} %fusion.35) | copy-start | bytes 196
  39.0 18.7 %copy-start.3 = (f32[16,8,64]{2,1,0:T(8,128)S(1)}, f32[16,8,64]{2,1,0:T(8,128)}, u32[]{:S(2)}) copy-start(f32[16,8,64]{2,1,0:T(8,128)} %get-tuple-element.29) | copy-start | bytes 98308
  39.0 18.7 %copy-start.4 = (f32[16,8]{1,0:T(8,128)S(1)}, f32[16,8]{1,0:T(8,128)}, u32[]{:S(2)}) copy-start(f32[16,8]{1,0:T(8,128)} %get-tuple-element.28) | copy-start | bytes 1540
  39.0 18.9 %copy-start.8 = (s32[16]{0:T(128)S(1)}, s32[16]{0:T(128)}, u32[]{:S(2)}) copy-start(s32[16]{0:T(128)} %copy-done.7) | copy-start | bytes 196
  44.4 9.8 %all-to-all-start.3 = ((f32[8,4,8]{2,1,0:T(4,128)}), f32[8,4,8]{2,1,0:T(4,128)S(1)}, u32[]{:S(2)}, u32[]{:S(2)}) async-start(f32[8,4,8]{2,1,0:T(4,128)} %bitcast.80), calls=%async_computation.3 | async-start | bytes 32768 | tf_op jit(solution)/shard_map/all_to_all | solution.py:105
  54.2 14.9 %all-to-all-start.2 = ((f32[32,8,512]{2,1,0:T(8,128)}), f32[32,8,512]{2,1,0:T(8,128)S(1)}, u32[]{:S(2)}, u32[]{:S(2)}) async-start(f32[32,8,512]{2,1,0:T(8,128)} %broadcast_select_fusion), calls=%async_computation.2 | async-start | bytes 1048576 | tf_op jit(solution)/shard_map/all_to_all | solution.py:106
where the time goes:
time: 71.5 us; the launch traced here: 70.8 us
  waiting for transfers between devices  21.9 us (31%)
  starting transfers between devices  18.1 us (25%)
  other arithmetic  13.9 us (19%)
  local copies, waits for them, and re-layouts  13 us (18%)
  matrix products  3.71 us (5%)
    all_to_all x1, waiting for transfers between devices, body(): lax.all_to_all(partials[2], ('prompt', 'sample'), split_axis=0, concat_ax...  8.26 us
    all_to_all x1, starting transfers between devices, body(): lax.all_to_all(fanned, ('prompt', 'sample'), split_axis=0, concat_axis=0,...  7.28 us
    select_n x1, other arithmetic, routing_tables(): local_prompt = slot_index % P_DEV  5.61 us
    all_to_all x1, waiting for transfers between devices, body(): lax.all_to_all(partials[0], ('prompt', 'sample'), split_axis=0, concat_ax...  5.34 us
    all_to_all x1, waiting for transfers between devices, body(): lax.all_to_all(partials[1], ('prompt', 'sample'), split_axis=0, concat_ax...  4.95 us
    all_to_all x1, starting transfers between devices, body(): lax.all_to_all(partials[0], ('prompt', 'sample'), split_axis=0, concat_ax...  3.95 us
    all_to_all x1, starting transfers between devices, body(): lax.all_to_all(partials[2], ('prompt', 'sample'), split_axis=0, concat_ax...  3.49 us
    all_to_all x1, starting transfers between devices, body(): lax.all_to_all(partials[1], ('prompt', 'sample'), split_axis=0, concat_ax...  3.33 us
  transfers between devices with their start and end apart: 4, of which 4 were waited for; matrix products, arithmetic and copies ran while one was open for 17% of the time, Pallas kernels for 0%

commit v1 on v0

v1 whole, which is shorter than its diff:
```python
import functools
import math

import jax
import jax.numpy as jnp
from jax import lax
from jax.experimental import pallas as pl
from jax.experimental.pallas import tpu as pltpu
from jax.sharding import PartitionSpec as P

DL = 512
DR = 64
QKN = 128
LANES = 128
TILE_ROWS = 128
LOG2E = 1.4426950408889634
MESH = pl.DeviceIdType.MESH
F32 = jnp.float32
BF16 = jnp.bfloat16


def dot_t(a, b):
    return lax.dot_general(a, b, (((1,), (1,)), ((), ())), preferred_element_type=F32)


def dot(a, b):
    return lax.dot_general(a, b, (((1,), (0,)), ((), ())), preferred_element_type=F32)


def split3(x):
    hi = x.astype(BF16)
    left = x - hi.astype(F32)
    mid = left.astype(BF16)
    low = (left - mid.astype(F32)).astype(BF16)
    return hi, mid, low


def kernel(
    nz,
    nx,
    own_count,
    heads,
    sends,
    q_ref,
    kv_hbm,
    suf_hbm,
    len_ref,
    sp_ref,
    slot_ref,
    out_ref,
    packed,
    recv,
    ret,
    got,
    kbuf,
    sbuf,
    unpack,
    suf_out,
    result,
    local_sem,
    q_send,
    q_recv,
    r_send,
    r_recv,
):
    z = lax.axis_index("prompt")
    x = lax.axis_index("sample")
    prompts, tokens, features = kbuf.shape
    suffix = sbuf.shape[0] // own_count
    rows = sends * heads
    cols = own_count * heads
    packed_rows = nz * rows
    factor = LOG2E / math.sqrt(QKN + DR)
    pairs = [(dz, dx) for dz in range(nz) for dx in range(nx)]
    pairs.sort(key=lambda p: (min(p[0], nz - p[0]) + min(p[1], nx - p[1]), p))

    def ahead(dz, dx):
        return {"prompt": lax.rem(z + dz, nz), "sample": lax.rem(x + dx, nx)}

    def behind(dz, dx):
        return {"prompt": lax.rem(z + nz - dz, nz), "sample": lax.rem(x + nx - dx, nx)}

    barrier = pltpu.get_barrier_semaphore()
    for dz, dx in pairs[1:]:
        pl.semaphore_signal(barrier, inc=1, device_id=ahead(dz, dx), device_id_type=MESH)
    suf_copy = pltpu.make_async_copy(suf_hbm, sbuf, local_sem.at[0])
    suf_copy.start()
    kv_copy = pltpu.make_async_copy(kv_hbm, kbuf, local_sem.at[1])
    kv_copy.start()

    first = (z * nx + x) * own_count
    lane = lax.broadcasted_iota(jnp.int32, (own_count, cols), 1)
    row = lax.broadcasted_iota(jnp.int32, (own_count, cols), 0)
    owner_row = jnp.zeros((own_count, cols), jnp.int32)
    owner_lane = jnp.zeros((own_count, cols), jnp.int32)
    lane1 = lane[:1]
    local_lane = jnp.zeros((1, cols), jnp.int32)
    len_lane = jnp.zeros((1, cols), jnp.int32)
    lo_lane = jnp.zeros((1, cols), jnp.int32)
    sample_lane = jnp.zeros((own_count, cols), jnp.int32)
    for j in range(own_count):
        slot = slot_ref[sp_ref[first + j]]
        owner = lax.rem(lax.div(slot, prompts) - z + nz, nz)
        here = (lane >= j * heads) & (lane < (j + 1) * heads)
        owner_row = jnp.where(row == j, owner, owner_row)
        owner_lane = jnp.where(here, owner, owner_lane)
        sample_lane = jnp.where(here, j, sample_lane)
        local_lane = jnp.where(here[:1], lax.rem(slot, prompts), local_lane)
        len_lane = jnp.where(here[:1], len_ref[j], len_lane)
        lo_lane = jnp.where(here[:1], j * suffix, lo_lane)
    earlier = (owner_row == owner_lane) & (row < sample_lane)
    rank = jnp.sum(jnp.where(earlier, 1.0, 0.0), axis=0, keepdims=True).astype(jnp.int32)
    place = (owner_lane[:1] * sends + rank) * heads + (lane1 - sample_lane[:1] * heads)
    hot = lax.broadcasted_iota(jnp.int32, (packed_rows, cols), 0) == place

    def to_rows(values):
        return jnp.sum(jnp.where(hot, values.astype(F32), 0.0), axis=1, keepdims=True)

    hot_f = jnp.where(hot, 1.0, 0.0)
    mine = dot(hot_f.astype(BF16), q_ref[...]).astype(BF16)
    tail = jnp.broadcast_to(to_rows(local_lane), (packed_rows, LANES)).astype(BF16)
    packed[:, :features] = mine
    packed[:, features:] = tail[:, : packed.shape[1] - features]
    recv[:rows] = packed[:rows]

    pl.semaphore_wait(barrier, nz * nx - 1)
    q_copies = []
    for k, (dz, dx) in enumerate(pairs):
        if k == 0:
            q_copies.append(None)
            continue
        copy = pltpu.make_async_remote_copy(
            src_ref=packed.at[pl.ds(dz * rows, rows)],
            dst_ref=recv.at[pl.ds(k * rows, rows)],
            send_sem=q_send.at[k],
            recv_sem=q_recv.at[k],
            device_id=ahead(dz, dx),
            device_id_type=MESH,
        )
        copy.start()
        q_copies.append(copy)

    unpack[...] = hot_f.T.astype(BF16)
    lo = to_rows(lo_lane).astype(jnp.int32)
    hi = to_rows(lo_lane + len_lane).astype(jnp.int32)
    suf_copy.wait()
    scores = dot_t(packed[:, :features], sbuf[...]) * factor
    key = lax.broadcasted_iota(jnp.int32, scores.shape, 1)
    scores = jnp.where((key >= lo) & (key < hi), scores, -1e30)
    suf_max = jnp.max(scores, axis=1, keepdims=True)
    weights = jnp.exp2(scores - suf_max)
    suf_sum = jnp.sum(weights, axis=1, keepdims=True)
    suf_out[...] = dot(weights.astype(BF16), sbuf[:, :DL])

    kv_copy.wait()
    step = max(1, TILE_ROWS // rows)
    r_copies = [None] * len(pairs)
    for begin in range(0, len(pairs), step):
        end = min(begin + step, len(pairs))
        for k in range(begin, end):
            if k:
                q_copies[k].wait_recv()
        span = pl.ds(begin * rows, (end - begin) * rows)
        asked = recv[span, :features]
        local = recv[span, features : features + 1].astype(F32)
        scores = dot_t(asked, kbuf[0])
        for p in range(1, prompts):
            scores = jnp.where(local == float(p), dot_t(asked, kbuf[p]), scores)
        scores = scores * factor
        row_max = jnp.max(scores, axis=1, keepdims=True)
        weights = jnp.exp2(scores - row_max)
        row_sum = jnp.sum(weights, axis=1, keepdims=True)
        total = None
        for p in range(prompts):
            part = jnp.where(local == float(p), weights, 0.0).astype(BF16)
            part = dot(part, kbuf[p, :, :DL])
            total = part if total is None else total + part
        lse = row_max + jnp.log(row_sum) * LOG2E
        ret[span, :DL] = (total / row_sum).astype(BF16)
        place_of = lax.broadcasted_iota(jnp.int32, ((end - begin) * rows, LANES), 1)
        top, mid, low = split3(lse)
        tail = jnp.where(place_of == 0, top.astype(F32), jnp.where(place_of == 1, mid.astype(F32), low.astype(F32)))
        ret[span, DL:] = tail.astype(BF16)
        for k in range(begin, end):
            dz, dx = pairs[k]
            if k == 0:
                got[:rows] = ret[:rows]
                continue
            copy = pltpu.make_async_remote_copy(
                src_ref=ret.at[pl.ds(k * rows, rows)],
                dst_ref=got.at[pl.ds(k * rows, rows)],
                send_sem=r_send.at[k],
                recv_sem=r_recv.at[k],
                device_id=behind(dz, dx),
                device_id_type=MESH,
            )
            copy.start()
            r_copies[k] = copy

    for k in range(1, len(pairs)):
        r_copies[k].wait_recv()
    for dz in range(nz):
        span = pl.ds(dz * rows, rows)
        at = slice(dz * rows, (dz + 1) * rows)
        parts = []
        top = suf_max[at]
        for k, pair in enumerate(pairs):
            if pair[0] == dz:
                tail = got[pl.ds(k * rows, rows), DL:].astype(F32)
                lse = tail[:, 0:1] + tail[:, 1:2] + tail[:, 2:3]
                parts.append((k, lse))
                top = jnp.maximum(top, lse)
        share = jnp.exp2(suf_max[at] - top)
        total = share * suf_sum[at]
        numerator = share * suf_out[span, :]
        for k, lse in parts:
            share = jnp.exp2(lse - top)
            total = total + share
            numerator = numerator + share * got[pl.ds(k * rows, rows), :DL].astype(F32)
        result[span, :] = (numerator / total).astype(BF16)
    out_ref[...] = dot(unpack[...], result[...]).astype(BF16)
    for k in range(1, len(pairs)):
        q_copies[k].wait_send()
        r_copies[k].wait_send()


def body(nz, nx, queries, prompt_cache, suffix_cache, suffix_len, sample_prompt, prompt_slot):
    own_count, heads, features = queries.shape
    prompts, tokens, _ = prompt_cache.shape
    suffix = suffix_cache.shape[1]
    sends = max(1, own_count // nz)
    devices = nz * nx
    cols = own_count * heads
    packed_rows = nz * sends * heads
    all_rows = devices * sends * heads
    wide = pl.cdiv(features + 1, LANES) * LANES
    vmem = pl.BlockSpec(memory_space=pltpu.VMEM)
    smem = pl.BlockSpec(memory_space=pltpu.SMEM)
    hbm = pl.BlockSpec(memory_space=pl.ANY)
    out = pl.pallas_call(
        functools.partial(kernel, nz, nx, own_count, heads, sends),
        out_shape=jax.ShapeDtypeStruct((cols, DL), BF16),
        in_specs=[vmem, hbm, hbm, smem, smem, smem],
        out_specs=vmem,
        scratch_shapes=[
            pltpu.VMEM((packed_rows, wide), BF16),
            pltpu.VMEM((all_rows, wide), BF16),
            pltpu.VMEM((all_rows, DL + LANES), BF16),
            pltpu.VMEM((all_rows, DL + LANES), BF16),
            pltpu.VMEM((prompts, tokens, features), BF16),
            pltpu.VMEM((own_count * suffix, features), BF16),
            pltpu.VMEM((cols, packed_rows), BF16),
            pltpu.VMEM((packed_rows, DL), F32),
            pltpu.VMEM((packed_rows, DL), BF16),
            pltpu.SemaphoreType.DMA((2,)),
            pltpu.SemaphoreType.DMA((devices,)),
            pltpu.SemaphoreType.DMA((devices,)),
            pltpu.SemaphoreType.DMA((devices,)),
            pltpu.SemaphoreType.DMA((devices,)),
        ],
        compiler_params=pltpu.CompilerParams(collective_id=0, has_side_effects=True),
        name="latent_decode",
    )(
        queries.reshape(cols, features),
        prompt_cache,
        suffix_cache.reshape(own_count * suffix, features),
        suffix_len,
        sample_prompt,
        prompt_slot,
    )
    return out.reshape(own_count, heads, DL)


def solution(mesh):
    return jax.shard_map(
        functools.partial(body, mesh.shape["prompt"], mesh.shape["sample"]),
        mesh=mesh,
        in_specs=(
            P(("groups", "prompt", "sample"), "head", None),
            P(("groups", "prompt"), "sample", None),
            P(("groups", "prompt", "sample"), None, None),
            P(("groups", "prompt", "sample")),
            P("groups"),
            P("groups"),
        ),
        out_specs=P(("groups", "prompt", "sample"), "head", None),
        check_vma=False,
    )
```

time: 71.5 us -> 29.4 us (0.41)
  Pallas kernels: 0 us -> 25.3 us
  waiting for transfers between devices: 21.9 us -> 0 us
  starting transfers between devices: 18.1 us -> 0 us
  other arithmetic: 13.9 us -> 0 us
  local copies, waits for them, and re-layouts: 13 us -> 3.98 us
  matrix products: 3.71 us -> 0 us
    pallas_call x0 -> x1, Pallas kernels: none -> 25.3 us  [body(): pl.pallas_call(functools.partial(kernel, nz, nx, own_count, heads, sends)...]
    all_to_all x4 -> x0, waiting for transfers between devices: 21.9 us -> none  [the longest x1 8.26 us: body(): lax.all_to_all(partials[2], ('prompt', 'sample'), split_axis=0, concat_ax...]
    all_to_all x4 -> x0, starting transfers between devices: 18.1 us -> none  [the longest x1 7.28 us: body(): lax.all_to_all(fanned, ('prompt', 'sample'), split_axis=0, concat_axis=0,...]
    gather x12 -> x0, local copies, waits for them, and re-layouts: 9.45 us -> none  [the longest x2 2.67 us: prefix_partials(): jnp.take(rows, source_row, axis=0)]
    select_n x13 -> x0, other arithmetic: 8.62 us -> none  [the longest x1 5.61 us: routing_tables(): local_prompt = slot_index % P_DEV]
    unnamed x20 -> x2, local copies, waits for them, and re-layouts: 0.05 us -> 3.98 us
    dot_general x4 -> x0, matrix products: 3.71 us -> none  [the longest x2 2.24 us: partial_softmax(): jnp.einsum(score_form, asked, keys, preferred_element_type=jnp.float32)]
    reduce_sum x7 -> x0, other arithmetic: 1.89 us -> none  [the longest x1 0.74 us: body(): prefix_sum = jnp.sum(back_sum * rescale, axis=1)]
  transfers between devices with their start and end apart: 4 -> 0, of which waited for: 4 -> 0; matrix products, arithmetic and copies ran while one was open for 17% -> 0% of each run, Pallas kernels for 0% -> 0%
where the time goes in v1:
time: 29.4 us; the launch traced here: 29.3 us
  Pallas kernels  25.3 us (86%)
  local copies, waits for them, and re-layouts  3.98 us (14%)
    pallas_call x1, Pallas kernels, body(): pl.pallas_call(functools.partial(kernel, nz, nx, own_count, heads, sends)...  25.3 us
    unnamed x2, local copies, waits for them, and re-layouts  3.98 us

profile of v1, /device:TPU:0, one launch (start us, length us, event | category | flops | bytes accessed | tf_op | source)
XLA Modules:
  0.0 29.3 jit_solution(7514767803994542171)
XLA Ops:
  0.0 2.4 %copy.7.kv_hbm = bf16[2,512,576]{2,1,0:T(8,128)(2,1)} copy(bf16[2,512,576]{1,2,0:T(8,128)(2,1)} %param.7) | data formatting | bytes 2359296 | tf_op args[1]
  2.4 25.3 %latent_decode.1 = bf16[128,512]{1,0:T(8,128)(2,1)} custom-call(bf16[128,576]{1,0:T(8,128)(2,1)} %bitcast.5, bf16[2,512,576]{2,1,0:T(8,128)(2,1)} %copy.7.kv_hbm, bf16[1024,576]{1,0:T(8,128)(2,1)} %bitcast.3, s32[16]{0:T(128)} %len_ref.1, s32[128]{0:T(128)} %sp_ref.1, s32[8]{0:T(128)} %slot_ref.1), custom_call_target="tpu_custom_call" | custom-call | tf_op jit(solution)/shard_map/latent_decode/pallas_call | solution.py:240
  27.7 1.6 %copy.9 = bf16[16,8,512]{2,1,0:T(8,128)(2,1)} copy(bf16[16,8,512]{2,1,0:T(8,128)(2,1)} %bitcast.4) | data formatting | bytes 262144

commit v2 on v1

--- a/solution.py
+++ b/solution.py
@@ -65,14 +65,14 @@
 ):
     z = lax.axis_index("prompt")
     x = lax.axis_index("sample")
-    prompts, tokens, features = kbuf.shape
+    prompts, features, tokens = kbuf.shape
     suffix = sbuf.shape[0] // own_count
     rows = sends * heads
     cols = own_count * heads
     packed_rows = nz * rows
     factor = LOG2E / math.sqrt(QKN + DR)
     pairs = [(dz, dx) for dz in range(nz) for dx in range(nx)]
-    pairs.sort(key=lambda p: (min(p[0], nz - p[0]) + min(p[1], nx - p[1]), p))
+    pairs.sort(key=lambda p: (-min(p[0], nz - p[0]) - min(p[1], nx - p[1]), p))
 
     def ahead(dz, dx):
         return {"prompt": lax.rem(z + dz, nz), "sample": lax.rem(x + dx, nx)}
@@ -81,7 +81,7 @@
         return {"prompt": lax.rem(z + nz - dz, nz), "sample": lax.rem(x + nx - dx, nx)}
 
     barrier = pltpu.get_barrier_semaphore()
-    for dz, dx in pairs[1:]:
+    for dz, dx in pairs[:-1]:
         pl.semaphore_signal(barrier, inc=1, device_id=ahead(dz, dx), device_id_type=MESH)
     suf_copy = pltpu.make_async_copy(suf_hbm, sbuf, local_sem.at[0])
     suf_copy.start()
@@ -121,12 +121,12 @@
     tail = jnp.broadcast_to(to_rows(local_lane), (packed_rows, LANES)).astype(BF16)
     packed[:, :features] = mine
     packed[:, features:] = tail[:, : packed.shape[1] - features]
-    recv[:rows] = packed[:rows]
+    recv[pl.ds((len(pairs) - 1) * rows, rows)] = packed[:rows]
 
     pl.semaphore_wait(barrier, nz * nx - 1)
     q_copies = []
     for k, (dz, dx) in enumerate(pairs):
-        if k == 0:
+        if k == len(pairs) - 1:
             q_copies.append(None)
             continue
         copy = pltpu.make_async_remote_copy(
@@ -158,14 +158,14 @@
     for begin in range(0, len(pairs), step):
         end = min(begin + step, len(pairs))
         for k in range(begin, end):
-            if k:
+            if k < len(pairs) - 1:
                 q_copies[k].wait_recv()
         span = pl.ds(begin * rows, (end - begin) * rows)
         asked = recv[span, :features]
         local = recv[span, features : features + 1].astype(F32)
-        scores = dot_t(asked, kbuf[0])
+        scores = dot(asked, kbuf[0])
         for p in range(1, prompts):
-            scores = jnp.where(local == float(p), dot_t(asked, kbuf[p]), scores)
+            scores = jnp.where(local == float(p), dot(asked, kbuf[p]), scores)
         scores = scores * factor
         row_max = jnp.max(scores, axis=1, keepdims=True)
         weights = jnp.exp2(scores - row_max)
@@ -173,7 +173,7 @@
         total = None
         for p in range(prompts):
             part = jnp.where(local == float(p), weights, 0.0).astype(BF16)
-            part = dot(part, kbuf[p, :, :DL])
+            part = dot_t(part, kbuf[p, :DL, :])
             total = part if total is None else total + part
         lse = row_max + jnp.log(row_sum) * LOG2E
         ret[span, :DL] = (total / row_sum).astype(BF16)
@@ -183,8 +183,8 @@
         ret[span, DL:] = tail.astype(BF16)
         for k in range(begin, end):
             dz, dx = pairs[k]
-            if k == 0:
-                got[:rows] = ret[:rows]
+            if k == len(pairs) - 1:
+                got[pl.ds(k * rows, rows)] = ret[pl.ds(k * rows, rows)]
                 continue
             copy = pltpu.make_async_remote_copy(
                 src_ref=ret.at[pl.ds(k * rows, rows)],
@@ -197,7 +197,7 @@
             copy.start()
             r_copies[k] = copy
 
-    for k in range(1, len(pairs)):
+    for k in range(len(pairs) - 1):
         r_copies[k].wait_recv()
     for dz in range(nz):
         span = pl.ds(dz * rows, rows)
@@ -219,7 +219,7 @@
             numerator = numerator + share * got[pl.ds(k * rows, rows), :DL].astype(F32)
         result[span, :] = (numerator / total).astype(BF16)
     out_ref[...] = dot(unpack[...], result[...]).astype(BF16)
-    for k in range(1, len(pairs)):
+    for k in range(len(pairs) - 1):
         q_copies[k].wait_send()
         r_copies[k].wait_send()
 
@@ -247,7 +247,7 @@
             pltpu.VMEM((all_rows, wide), BF16),
             pltpu.VMEM((all_rows, DL + LANES), BF16),
             pltpu.VMEM((all_rows, DL + LANES), BF16),
-            pltpu.VMEM((prompts, tokens, features), BF16),
+            pltpu.VMEM((prompts, features, tokens), BF16),
             pltpu.VMEM((own_count * suffix, features), BF16),
             pltpu.VMEM((cols, packed_rows), BF16),
             pltpu.VMEM((packed_rows, DL), F32),
@@ -262,7 +262,7 @@
         name="latent_decode",
     )(
         queries.reshape(cols, features),
-        prompt_cache,
+        jnp.swapaxes(prompt_cache, 1, 2),
         suffix_cache.reshape(own_count * suffix, features),
         suffix_len,
         sample_prompt,

time: 29.4 us -> 25 us (0.85)
  local copies, waits for them, and re-layouts: 3.98 us -> 1.57 us
  Pallas kernels: 25.3 us -> 23.3 us
    unnamed x2 -> x1, local copies, waits for them, and re-layouts: 3.98 us -> 1.57 us
    pallas_call x1, Pallas kernels: 25.3 us -> 23.3 us  [body(): pl.pallas_call(functools.partial(kernel, nz, nx, own_count, heads, sends)...]
where the time goes in v2:
time: 25 us; the launch traced here: 24.8 us
  Pallas kernels  23.3 us (93%)
  local copies, waits for them, and re-layouts  1.57 us (6%)
    pallas_call x1, Pallas kernels, body(): pl.pallas_call(functools.partial(kernel, nz, nx, own_count, heads, sends)...  23.3 us
    unnamed x1, local copies, waits for them, and re-layouts  1.57 us

profile of v2, /device:TPU:0, one launch (start us, length us, event | category | flops | bytes accessed | tf_op | source)
XLA Modules:
  0.0 24.8 jit_solution(7039577313397737190)
XLA Ops:
  0.0 23.3 %latent_decode.1 = bf16[128,512]{1,0:T(8,128)(2,1)} custom-call(bf16[128,576]{1,0:T(8,128)(2,1)} %bitcast.7, bf16[2,576,512]{2,1,0:T(8,128)(2,1)} %bitcast.5, bf16[1024,576]{1,0:T(8,128)(2,1)} %bitcast.4, s32[16]{0:T(128)} %len_ref.1, s32[128]{0:T(128)} %sp_ref.1, s32[8]{0:T(128)} %slot_ref.1), custom_call_target="tpu_custom_call" | custom-call | tf_op jit(solution)/shard_map/latent_decode/pallas_call | solution.py:240
  23.3 1.6 %copy.8 = bf16[16,8,512]{2,1,0:T(8,128)(2,1)} copy(bf16[16,8,512]{2,1,0:T(8,128)(2,1)} %bitcast.6) | data formatting | bytes 262144

commit v3 on v2

--- a/solution.py
+++ b/solution.py
@@ -41,17 +41,21 @@
     own_count,
     heads,
     sends,
-    q_ref,
+    q_hbm,
     kv_hbm,
     suf_hbm,
-    len_ref,
-    sp_ref,
-    slot_ref,
+    len_hbm,
+    sp_hbm,
+    slot_hbm,
     out_ref,
     packed,
     recv,
     ret,
     got,
+    len_ref,
+    sp_ref,
+    slot_ref,
+    q_ref,
     kbuf,
     sbuf,
     unpack,
@@ -83,11 +87,21 @@
     barrier = pltpu.get_barrier_semaphore()
     for dz, dx in pairs[:-1]:
         pl.semaphore_signal(barrier, inc=1, device_id=ahead(dz, dx), device_id_type=MESH)
+    tables = [
+        pltpu.make_async_copy(source, target, local_sem.at[3 + i])
+        for i, (source, target) in enumerate(((slot_hbm, slot_ref), (sp_hbm, sp_ref), (len_hbm, len_ref)))
+    ]
+    for table in tables:
+        table.start()
+    q_load = pltpu.make_async_copy(q_hbm, q_ref, local_sem.at[2])
+    q_load.start()
     suf_copy = pltpu.make_async_copy(suf_hbm, sbuf, local_sem.at[0])
     suf_copy.start()
     kv_copy = pltpu.make_async_copy(kv_hbm, kbuf, local_sem.at[1])
     kv_copy.start()
 
+    for table in tables:
+        table.wait()
     first = (z * nx + x) * own_count
     lane = lax.broadcasted_iota(jnp.int32, (own_count, cols), 1)
     row = lax.broadcasted_iota(jnp.int32, (own_count, cols), 0)
@@ -117,6 +131,7 @@
         return jnp.sum(jnp.where(hot, values.astype(F32), 0.0), axis=1, keepdims=True)
 
     hot_f = jnp.where(hot, 1.0, 0.0)
+    q_load.wait()
     mine = dot(hot_f.astype(BF16), q_ref[...]).astype(BF16)
     tail = jnp.broadcast_to(to_rows(local_lane), (packed_rows, LANES)).astype(BF16)
     packed[:, :features] = mine
@@ -235,24 +250,27 @@
     all_rows = devices * sends * heads
     wide = pl.cdiv(features + 1, LANES) * LANES
     vmem = pl.BlockSpec(memory_space=pltpu.VMEM)
-    smem = pl.BlockSpec(memory_space=pltpu.SMEM)
     hbm = pl.BlockSpec(memory_space=pl.ANY)
     out = pl.pallas_call(
         functools.partial(kernel, nz, nx, own_count, heads, sends),
-        out_shape=jax.ShapeDtypeStruct((cols, DL), BF16),
-        in_specs=[vmem, hbm, hbm, smem, smem, smem],
+        out_shape=pltpu.VMEM((cols, DL), BF16),
+        in_specs=[hbm] * 6,
         out_specs=vmem,
         scratch_shapes=[
             pltpu.VMEM((packed_rows, wide), BF16),
             pltpu.VMEM((all_rows, wide), BF16),
             pltpu.VMEM((all_rows, DL + LANES), BF16),
             pltpu.VMEM((all_rows, DL + LANES), BF16),
+            pltpu.SMEM(suffix_len.shape, jnp.int32),
+            pltpu.SMEM(sample_prompt.shape, jnp.int32),
+            pltpu.SMEM(prompt_slot.shape, jnp.int32),
+            pltpu.VMEM((cols, features), BF16),
             pltpu.VMEM((prompts, features, tokens), BF16),
             pltpu.VMEM((own_count * suffix, features), BF16),
             pltpu.VMEM((cols, packed_rows), BF16),
             pltpu.VMEM((packed_rows, DL), F32),
             pltpu.VMEM((packed_rows, DL), BF16),
-            pltpu.SemaphoreType.DMA((2,)),
+            pltpu.SemaphoreType.DMA((6,)),
             pltpu.SemaphoreType.DMA((devices,)),
             pltpu.SemaphoreType.DMA((devices,)),
             pltpu.SemaphoreType.DMA((devices,)),

time: 25 us -> 22.5 us (0.900)
  Pallas kernels: 23.3 us -> 21.7 us
  local copies, waits for them, and re-layouts: 1.57 us -> 0.66 us
    pallas_call x1, Pallas kernels: 23.3 us -> 21.7 us  [body(): pl.pallas_call(functools.partial(kernel, nz, nx, own_count, heads, sends)...]
    unnamed x1, local copies, waits for them, and re-layouts: 1.57 us -> 0.66 us
where the time goes in v3:
time: 22.5 us; the launch traced here: 22.4 us
  Pallas kernels  21.7 us (96%)
  local copies, waits for them, and re-layouts  0.66 us (3%)
    pallas_call x1, Pallas kernels, body(): pl.pallas_call(functools.partial(kernel, nz, nx, own_count, heads, sends)...  21.7 us
    unnamed x1, local copies, waits for them, and re-layouts  0.66 us

profile of v3, /device:TPU:0, one launch (start us, length us, event | category | flops | bytes accessed | tf_op | source)
XLA Modules:
  0.0 22.4 jit_solution(18308915992961268677)
XLA Ops:
  0.0 21.7 %latent_decode.1 = bf16[128,512]{1,0:T(8,128)(2,1)S(1)} custom-call(bf16[128,576]{1,0:T(8,128)(2,1)} %bitcast.7, bf16[2,576,512]{2,1,0:T(8,128)(2,1)} %bitcast.6, bf16[1024,576]{1,0:T(8,128)(2,1)} %bitcast.5, s32[16]{0:T(128)} %len_hbm.1, s32[128]{0:T(128)} %sp_hbm.1, s32[8]{0:T(128)} %slot_hbm.1), custom_call_target="tpu_custom_call" | custom-call | tf_op jit(solution)/shard_map/latent_decode/pallas_call | solution.py:254
  21.7 0.7 %copy.8 = bf16[16,8,512]{2,1,0:T(8,128)(2,1)} copy(bf16[16,8,512]{2,1,0:T(8,128)(2,1)S(1)} %bitcast.4) | data formatting | bytes 262144

commit v4 on v3

--- a/solution.py
+++ b/solution.py
@@ -76,7 +76,7 @@
     packed_rows = nz * rows
     factor = LOG2E / math.sqrt(QKN + DR)
     pairs = [(dz, dx) for dz in range(nz) for dx in range(nx)]
-    pairs.sort(key=lambda p: (-min(p[0], nz - p[0]) - min(p[1], nx - p[1]), p))
+    pairs.sort(key=lambda p: (-min(p[0], nz - p[0]), -min(p[1], nx - p[1]), p))
 
     def ahead(dz, dx):
         return {"prompt": lax.rem(z + dz, nz), "sample": lax.rem(x + dx, nx)}
@@ -212,9 +212,10 @@
             copy.start()
             r_copies[k] = copy
 
-    for k in range(len(pairs) - 1):
-        r_copies[k].wait_recv()
-    for dz in range(nz):
+    for dz in sorted(range(nz), key=lambda dz: (-min(dz, nz - dz), dz)):
+        for k, pair in enumerate(pairs[:-1]):
+            if pair[0] == dz:
+                r_copies[k].wait_recv()
         span = pl.ds(dz * rows, rows)
         at = slice(dz * rows, (dz + 1) * rows)
         parts = []

time: 22.5 us -> 22.3 us (level)
    pallas_call x1, Pallas kernels: 21.7 us -> 21.5 us  [body(): pl.pallas_call(functools.partial(kernel, nz, nx, own_count, heads, sends)...]
where the time goes in v4:
time: 22.3 us; the launch traced here: 22.1 us
  Pallas kernels  21.5 us (96%)
  local copies, waits for them, and re-layouts  0.66 us (3%)
    pallas_call x1, Pallas kernels, body(): pl.pallas_call(functools.partial(kernel, nz, nx, own_count, heads, sends)...  21.5 us
    unnamed x1, local copies, waits for them, and re-layouts  0.66 us

profile of v4, /device:TPU:0, one launch (start us, length us, event | category | flops | bytes accessed | tf_op | source)
XLA Modules:
  0.0 22.1 jit_solution(8305073344973106740)
XLA Ops:
  0.0 21.5 %latent_decode.1 = bf16[128,512]{1,0:T(8,128)(2,1)S(1)} custom-call(bf16[128,576]{1,0:T(8,128)(2,1)} %bitcast.7, bf16[2,576,512]{2,1,0:T(8,128)(2,1)} %bitcast.6, bf16[1024,576]{1,0:T(8,128)(2,1)} %bitcast.5, s32[16]{0:T(128)} %len_hbm.1, s32[128]{0:T(128)} %sp_hbm.1, s32[8]{0:T(128)} %slot_hbm.1), custom_call_target="tpu_custom_call" | custom-call | tf_op jit(solution)/shard_map/latent_decode/pallas_call | solution.py:255
  21.5 0.7 %copy.8 = bf16[16,8,512]{2,1,0:T(8,128)(2,1)} copy(bf16[16,8,512]{2,1,0:T(8,128)(2,1)S(1)} %bitcast.4) | data formatting | bytes 262144
